TPU v7x, 512 devices: a whole 4x4x16 slice. The times are simulated.
512 devices in a mesh: seq: 128 (over z, y, core), head: 4 (over x).
Axes of the slice: x: 4, y: 4, z: 16, core: 2. Of those that a mesh axis runs over, the one named last changes fastest.
Arguments:
- queries: bfloat16 [65536, 2048], P('seq', 'head'), may hold values from -6 to 6
- key_vectors: bfloat16 [65536, 2048], P('seq', 'head'), may hold values from -6 to 6
- value_vectors: bfloat16 [65536, 2048], P('seq', 'head'), may hold values from -6 to 6
- gate_input: bfloat16 [65536, 2048], P('seq', 'head'), may hold values from -6 to 6
- out_weight: bfloat16 [2048, 4096], P('seq', 'head'), may hold values from -0.125 to 0.125
Outputs:
- layer_output: bfloat16 [65536, 4096], P('seq', 'head')
All inputs are finite; a program needn't handle non-finite values.
Results may differ from a plain program's by a relative error of at most 0.0057.
Values may be sent and summed in bfloat16 or wider, within the bound.
No kernel may reach another device: no remote copies, remote signals or barrier semaphores. Data moves between devices by JAX's collectives and lax.ppermute only.
A program may use at most 64 MiB of HBM per device.

v0:
```python
import jax
import jax.numpy as jnp
from jax import lax
from jax.sharding import Mesh
from jax.sharding import PartitionSpec as P

HD = 128
SEQ = ("seq_0", "seq_1", "seq_2")


def nothing_yet(shard, identity):
    return jnp.broadcast_to(jnp.asarray(identity, shard.dtype), shard.shape)


def carried_in(shard, axes, combine, identity):
    before = start = nothing_yet(shard, identity)
    total = shard
    for axis in reversed(axes):
        count, position = (lax.axis_size(axis), lax.axis_index(axis))
        pieces = lax.all_gather(total, axis)
        inside, total = (start, start)
        for k in range(count):
            passed = k < position
            total = combine(total, pieces[k])
            inside = jnp.where(passed, total, inside)
        before = combine(inside, before)
    return before


def sent_to_all(shard, axis):
    count = lax.axis_size(axis)
    return lax.all_to_all(
        jnp.broadcast_to(shard[None], (count, *shard.shape)), axis, 0, 0, tiled=True
    )


def of_everyone(shard, axis):
    everything = sent_to_all(shard, axis)
    return jnp.sum(everything, axis=0)


def in_order(blocks, dim):
    shape = list(blocks.shape[1:])
    shape[dim] *= blocks.shape[0]
    return jnp.moveaxis(blocks, 0, dim).reshape(shape)


def gather_directly(shard, axis, dim):
    blocks = sent_to_all(shard, axis)
    return in_order(blocks, dim)


def stacked_from(shard, axes, sequence):
    blocks = shard[None]
    for k in sequence:
        blocks = lax.all_gather(blocks, axes[k], axis=0, tiled=True)
    block = [lax.axis_size(axes[k]) for k in reversed(sequence)]
    blocks = blocks.reshape(*block, *shard.shape)
    turned = sorted(range(len(sequence)), key=lambda place: sequence[len(sequence) - 1 - place])
    return blocks.transpose(*turned, *range(len(sequence), blocks.ndim)).reshape(-1, *shard.shape)


def gathered_by_axis(shard, axes, sequence, dim):
    return in_order(stacked_from(shard, axes, sequence), dim)


def add_states(earlier, later):
    return earlier + later


def carried(own_state):
    return carried_in(own_state, SEQ, add_states, jnp.zeros_like(own_state))


def in_shard(qhead, khead, vhead, scale):
    rows = qhead.shape[0]
    step = min(rows, 512)
    scores = jnp.einsum("thd,shd->hts", qhead, khead, preferred_element_type=jnp.float32) * scale
    rowpos = 0 + lax.broadcasted_iota(jnp.int32, (step, step), 0)
    colpos = lax.broadcasted_iota(jnp.int32, (step, step), 1)
    scores = jnp.where((colpos <= rowpos)[None, :, :], scores, 0.0).astype(jnp.bfloat16)
    pieces = jnp.einsum("hts,she->the", scores, vhead, preferred_element_type=jnp.float32)
    return pieces


def per_device(queries, key_vectors, value_vectors, gate_input, out_weight):
    rows, width = queries.shape
    heads = width // HD
    scale = HD ** (-0.5)
    qhead = queries.reshape(rows, heads, HD)
    khead = key_vectors.reshape(rows, heads, HD)
    vhead = value_vectors.reshape(rows, heads, HD)
    own_state = jnp.einsum("thd,the->hde", khead, vhead, preferred_element_type=jnp.float32)
    local = in_shard(qhead, khead, vhead, scale)
    prefix = carried(own_state)
    inter = (
        jnp.einsum(
            "thd,hde->the", qhead, prefix.astype(jnp.bfloat16), preferred_element_type=jnp.float32
        )
        * scale
    )
    attn = (local + inter).reshape(rows, width)
    squares = jnp.sum(attn * attn, axis=1)
    hidden = (attn * jax.nn.silu(gate_input.astype(jnp.float32))).astype(jnp.bfloat16)
    total = of_everyone(squares, "head")
    features = gather_directly(hidden, "head", 1)
    full_block = gathered_by_axis(out_weight, SEQ, (1, 0, 2), 0)
    projected = jnp.dot(features, full_block, preferred_element_type=jnp.float32)
    mean_square = total / features.shape[1]
    return (projected * lax.rsqrt(mean_square + 1e-06)[:, None]).astype(jnp.bfloat16)


def solution(mesh):
    torus = Mesh(
        mesh.devices.reshape(16, 4, 2, mesh.shape["head"]), ("seq_0", "seq_1", "seq_2", "head")
    )
    return jax.shard_map(
        per_device,
        mesh=torus,
        in_specs=(P(SEQ, "head"), P(SEQ, "head"), P(SEQ, "head"), P(SEQ, "head"), P(SEQ, "head")),
        out_specs=P(SEQ, "head"),
        check_vma=False,
    )
```

profile of v0, /device:TPU:8, one launch (start us, length us, event | category | flops | bytes accessed | tf_op | source)
XLA Modules:
  0.0 251.4 jit_solution(18268697951905926214)
XLA Ops:
  6.5 1.3 copy.62
  7.9 1.3 fusion.10
  9.2 2.2 all-gather
  11.4 0.7 slice_add_fusion.18
  12.2 15.3 %all-gather.1 = bf16[64,1024]{1,0:T(8,128)(2,1)} all-gather(bf16[16,1024]{1,0:T(8,128)(2,1)S(1)} %copy-done.3), channel_id=3, replica_groups=mesh['seq_0'=16,'seq_1'=4,'seq_2'=2,'head'=4] {'seq_1'}, dimensions={0}, use_global_device_ids=true | all-gather | bytes 163840 | tf_op jit(solution)/shard_map/all_gather | solution.py:56
  27.6 19.7 %all-gather.14.cloned.1.call-done = f32[16,128,128]{2,1,0:T(8,128)} async-done(((f32[4,128,128]{2,1,0:T(8,128)}), f32[16,128,128]{2,1,0:T(8,128)}) %all-gather.14.cloned.1.call-update) | async-done | bytes 1048592 | tf_op jit(solution)/shard_map/all_gather | solution.py:20
  47.3 1.9 fusion.24
  49.3 74.3 %all-gather.10.cloned.1.call-done = bf16[64,16,1024]{2,1,0:T(8,128)(2,1)} async-done(((bf16[4,16,1024]{2,1,0:T(8,128)(2,1)}), bf16[64,16,1024]{2,1,0:T(8,128)(2,1)}) %all-gather.10.cloned.1.call-update) | async-done | bytes 2097168 | tf_op jit(solution)/shard_map/all_gather | solution.py:56
  123.7 0.1 iota_compare_fusion
  123.8 76.8 %all-gather.8.cloned.1.call-done = f32[16,4,128,128]{3,2,1,0:T(8,128)} async-done(((f32[1,4,128,128]{3,2,1,0:T(8,128)}), f32[16,4,128,128]{3,2,1,0:T(8,128)}) %all-gather.8.cloned.1.call-update) | async-done | bytes 4194320 | tf_op jit(solution)/shard_map/all_gather | solution.py:20
  200.6 4.0 %fusion.3 = f32[512,4,128]{0,2,1:T(8,128)} fusion(f32[16,4,128,128]{3,2,1,0:T(8,128)} %all-gather.8.cloned.1.call-done, f32[1,4,128,128]{3,2,1,0:T(8,128)} %fusion.24, f32[4,128,128]{2,1,0:T(8,128)S(1)} %copy-done.1, f32[16,128,128]{2,1,0:T(8,128)} %all-gather.14.cloned.1.call-done, f32[8,128,128]{2,1,0:T(8,128)S(1)} %all-gather, pred[]{:T(512)S(6)} %gt.66, ...), kind=kOutput, calls=%fused_computation.6 | convolution fusion | flops 70123520 | bytes 7340054 | tf_op jit(solution)/shard_map/thd,hde->the/dot_general | solution.py:97
  204.6 2.6 %multiply_reduce_fusion = (f32[512]{0:T(512)S(1)}, f32[512,4,128]{0,2,1:T(8,128)S(1)}) fusion(f32[512,4,128]{0,2,1:T(8,128)} %fusion.3, bf16[512,4,128]{0,2,1:T(8,128)(2,1)S(1)} %bitcast.76, pred[512,512]{1,0:T(8,128)(4,1)S(1)} %iota_compare_fusion, bf16[512,512]{1,0:T(8,128)(2,1)S(1)} %copy-done.2, bf16[512,512]{1,0:T(8,128)(2,1)S(1)} %copy-done), kind=kOutput, calls=%fused_computation.13 | convolution fusion | flops 540802560 | bytes 3934208 | tf_op jit(solution)/shard_map/hts,she->the/dot_general | solution.py:82
  207.2 0.3 copy.56
  207.6 0.6 broadcast_in_dim.37
  208.2 4.3 %all-to-all-start.1 = ((f32[4,1,512]{2,1,0:T(1,128)}), f32[4,1,512]{2,1,0:T(1,128)S(1)}, u32[]{:S(2)}, u32[]{:S(2)}) async-start(f32[4,1,512]{2,1,0:T(1,128)} %broadcast_in_dim.37), calls=%async_computation.1 | async-start | bytes 16384 | tf_op jit(solution)/shard_map/all_to_all | solution.py:32
  212.4 1.4 fusion.8
  213.8 0.2 copy.57
  214.0 3.8 %all-to-all-done.1 = f32[4,1,512]{2,1,0:T(1,128)S(1)} async-done(((f32[4,1,512]{2,1,0:T(1,128)}), f32[4,1,512]{2,1,0:T(1,128)S(1)}, u32[]{:S(2)}, u32[]{:S(2)}) %all-to-all-start.1) | async-done | bytes 8224 | tf_op jit(solution)/shard_map/all_to_all | solution.py:32
  217.8 1.5 broadcast_in_dim.35
  219.3 3.6 %all-to-all-start = ((bf16[4,512,512]{1,2,0:T(8,128)(2,1)}), bf16[4,512,512]{1,2,0:T(8,128)(2,1)S(1)}, u32[]{:S(2)}, u32[]{:S(2)}) async-start(bf16[4,512,512]{1,2,0:T(8,128)(2,1)} %broadcast_in_dim.35), calls=%async_computation | async-start | bytes 4194304 | tf_op jit(solution)/shard_map/all_to_all | solution.py:32
  222.9 0.3 all-gather.12.cloned.1.call-done
  223.2 5.0 %copy.58 = bf16[16,4,2,16,1024]{4,3,2,1,0:T(8,128)(2,1)} copy(bf16[16,4,2,16,1024]{4,3,1,0,2:T(8,128)(2,1)} %bitcast.72) | data formatting | bytes 8388608 | tf_op jit(solution)/shard_map/transpose | solution.py:60
  228.2 11.2 %all-to-all-done = bf16[4,512,512]{1,2,0:T(8,128)(2,1)S(1)} async-done(((bf16[4,512,512]{1,2,0:T(8,128)(2,1)}), bf16[4,512,512]{1,2,0:T(8,128)(2,1)S(1)}, u32[]{:S(2)}, u32[]{:S(2)}) %all-to-all-start) | async-done | bytes 2097184 | tf_op jit(solution)/shard_map/all_to_all | solution.py:32
  239.4 5.5 %multiply_convert_fusion = bf16[512,1024]{1,0:T(8,128)(2,1)} fusion(bf16[512,2048]{0,1:T(8,128)(2,1)S(1)} %bitcast.74, bf16[2048,1024]{1,0:T(8,128)(2,1)} %bitcast.73, f32[512]{0:T(512)S(1)} %add_rsqrt_fusion), kind=kOutput, calls=%fused_computation.1 | convolution fusion | flops 2148532224 | bytes 7342080 | tf_op jit(solution)/shard_map/dot_general | solution.py:108
  (18 shorter events, 0.2 us)
Async XLA Ops:
  6.5 194.1 %copy-start = (bf16[512,512]{1,0:T(8,128)(2,1)S(1)}, bf16[512,512]{1,0:T(8,128)(2,1)}, u32[]{:S(2)}) copy-start(bf16[512,512]{1,0:T(8,128)(2,1)} %param.5) | copy-start | bytes 1572868
  6.5 5.7 %copy-start.3 = (bf16[16,1024]{1,0:T(8,128)(2,1)S(1)}, bf16[16,1024]{1,0:T(8,128)(2,1)}, u32[]{:S(2)}) copy-start(bf16[16,1024]{1,0:T(8,128)(2,1)} %param.9) | copy-start | bytes 98308
  6.5 40.8 %all-gather.14.cloned.1.call-start = ((), (), s32[]{:S(2)}) async-start(), calls=%async_computation.5 | async-start | bytes 1310720 | tf_op jit(solution)/shard_map/all_gather | solution.py:20
  12.1 188.5 %copy-start.1 = (f32[4,128,128]{2,1,0:T(8,128)S(1)}, f32[4,128,128]{2,1,0:T(8,128)}, u32[]{:S(2)}) copy-start(f32[4,128,128]{2,1,0:T(8,128)} %slice_add_fusion.18) | copy-start | bytes 786436
  12.1 111.5 %all-gather.10.cloned.1.call-start = ((), (), s32[]{:S(2)}) async-start(), calls=%async_computation.3 | async-start | bytes 2228224 | tf_op jit(solution)/shard_map/all_gather | solution.py:56
  27.5 173.1 %all-gather.8.cloned.1.call-start = ((), (), s32[]{:S(2)}) async-start(), calls=%async_computation.2 | async-start | bytes 4456448 | tf_op jit(solution)/shard_map/all_gather | solution.py:20
  49.3 155.4 %copy-start.2 = (bf16[512,512]{1,0:T(8,128)(2,1)S(1)}, bf16[512,512]{1,0:T(8,128)(2,1)}, u32[]{:S(2)}) copy-start(bf16[512,512]{1,0:T(8,128)(2,1)} %param.7) | copy-start | bytes 1572868
  49.3 173.9 %all-gather.12.cloned.1.call-start = ((), (), s32[]{:S(2)}) async-start(), calls=%async_computation.4 | async-start | bytes 6291456 | tf_op jit(solution)/shard_map/all_gather | solution.py:56
  208.2 9.6 %all-to-all-start.1 = ((f32[4,1,512]{2,1,0:T(1,128)}), f32[4,1,512]{2,1,0:T(1,128)S(1)}, u32[]{:S(2)}, u32[]{:S(2)}) async-start(f32[4,1,512]{2,1,0:T(1,128)} %broadcast_in_dim.37), calls=%async_computation.1 | async-start | bytes 16384 | tf_op jit(solution)/shard_map/all_to_all | solution.py:32
  219.3 20.1 %all-to-all-start = ((bf16[4,512,512]{1,2,0:T(8,128)(2,1)}), bf16[4,512,512]{1,2,0:T(8,128)(2,1)S(1)}, u32[]{:S(2)}, u32[]{:S(2)}) async-start(bf16[4,512,512]{1,2,0:T(8,128)(2,1)} %broadcast_in_dim.35), calls=%async_computation | async-start | bytes 4194304 | tf_op jit(solution)/shard_map/all_to_all | solution.py:32
Sparse Core Ops, SparseCore 0:
  12.3 34.9 all-gather.13
  49.4 74.1 all-gather.9
  125.7 74.8 all-gather.7
  202.6 20.5 all-gather.11
where the time goes:
time: 252 us; the launch traced here: 251 us
  waiting for transfers between devices  186 us (74%)
  blocking collectives  17.5 us (7%)
  matrix products  13.4 us (5%)
  between operations  13.2 us (5%)
  local copies, waits for them, and re-layouts  8.97 us (4%)
  starting transfers between devices  8 us (3%)
  other arithmetic  4.14 us (2%)
    all_gather x2, waiting for transfers between devices, carried_in(): pieces = lax.all_gather(total, axis)  96.6 us
    all_gather x2, waiting for transfers between devices, stacked_from(): blocks = lax.all_gather(blocks, axes[k], axis=0, tiled=True)  74.5 us
    all_gather x1, blocking collectives, stacked_from(): blocks = lax.all_gather(blocks, axes[k], axis=0, tiled=True)  15.3 us
    all_to_all x2, waiting for transfers between devices, sent_to_all(): lax.all_to_all(jnp.broadcast_to(shard[None], (count, *shard.shape)), axis...  15 us
    all_to_all x2, starting transfers between devices, sent_to_all(): lax.all_to_all(jnp.broadcast_to(shard[None], (count, *shard.shape)), axis...  7.87 us
    dot_general x1, matrix products, per_device(): jnp.dot(features, full_block, preferred_element_type=jnp.float32)  5.51 us
  transfers between devices with their start and end apart: 6, of which 6 were waited for; matrix products, arithmetic and copies ran while one was open for 7% of the time, Pallas kernels for 0%

commit v1 on v0

--- a/solution.py
+++ b/solution.py
@@ -53,7 +53,9 @@
 def stacked_from(shard, axes, sequence):
     blocks = shard[None]
     for k in sequence:
-        blocks = lax.all_gather(blocks, axes[k], axis=0, tiled=True)
+        blocks = jnp.concatenate(
+            lax.all_to_all(jnp.stack([blocks] * lax.axis_size(axes[k])), axes[k], 0, 0), axis=0
+        )
     block = [lax.axis_size(axes[k]) for k in reversed(sequence)]
     blocks = blocks.reshape(*block, *shard.shape)
     turned = sorted(range(len(sequence)), key=lambda place: sequence[len(sequence) - 1 - place])

time: 252 us -> 239 us (0.948)
  the two profiles are of different devices: /device:TPU:8 before, /device:TPU:2 now
where the time goes in v1:
time: 239 us
  waiting for transfers between devices  152 us (64%)
  starting transfers between devices  30.8 us (13%)
  matrix products  13.8 us (6%)
  between operations  13.6 us (6%)
  blocking collectives  12.4 us (5%)
  local copies, waits for them, and re-layouts  10.6 us (4%)
  other arithmetic  5.45 us (2%)
    all_to_all x2, waiting for transfers between devices, stacked_from(): lax.all_to_all(jnp.stack([blocks] * lax.axis_size(axes[k])), axes[k], 0, 0)  97.9 us
    all_gather x2, waiting for transfers between devices, carried_in(): pieces = lax.all_gather(total, axis)  37.8 us
    all_to_all x2, starting transfers between devices, stacked_from(): lax.all_to_all(jnp.stack([blocks] * lax.axis_size(axes[k])), axes[k], 0, 0)  20.9 us
    all_to_all x2, waiting for transfers between devices, sent_to_all(): lax.all_to_all(jnp.broadcast_to(shard[None], (count, *shard.shape)), axis...  16.2 us
    all_to_all x1, blocking collectives, stacked_from(): lax.all_to_all(jnp.stack([blocks] * lax.axis_size(axes[k])), axes[k], 0, 0)  10.2 us
    all_to_all x2, starting transfers between devices, sent_to_all(): lax.all_to_all(jnp.broadcast_to(shard[None], (count, *shard.shape)), axis...  9.86 us
    dot_general x1, matrix products, per_device(): jnp.dot(features, full_block, preferred_element_type=jnp.float32)  5.51 us
    all_to_all x1, local copies, waits for them, and re-layouts, stacked_from(): lax.all_to_all(jnp.stack([blocks] * lax.axis_size(axes[k])), axes[k], 0, 0)  5.01 us
  transfers between devices with their start and end apart: 6, of which 5 were waited for; matrix products, arithmetic and copies ran while one was open for 8% of the time, Pallas kernels for 0%

profile of v1, /device:TPU:2, one launch (start us, length us, event | category | flops | bytes accessed | tf_op | source)
XLA Modules:
  0.0 238.8 jit_solution(17685651609442065567)
XLA Ops:
  6.5 1.3 copy.52
  7.9 1.5 fusion.10
  9.4 2.2 all-gather
  11.6 0.7 slice_add_fusion.18
  12.4 10.2 %all_to_all.26 = bf16[4,1,16,1024]{3,2,1,0:T(8,128)(2,1)S(1)} all-to-all(bf16[4,1,16,1024]{3,2,1,0:T(8,128)(2,1)S(1)} %stack.9), channel_id=1, replica_groups=mesh['seq_0'=16,'seq_1'=4,'seq_2'=2,'head'=4] {'seq_1'}, dimensions={0} | all-to-all | bytes 262144 | tf_op jit(solution)/shard_map/all_to_all | solution.py:57
  22.6 1.6 stack.10
  24.2 15.2 %all-to-all-start.2 = ((bf16[16,4,16,1024]{3,2,1,0:T(8,128)(2,1)}), bf16[16,4,16,1024]{3,2,1,0:T(8,128)(2,1)S(1)}, u32[]{:S(2)}, u32[]{:S(2)}) async-start(bf16[16,4,16,1024]{3,2,1,0:T(8,128)(2,1)} %stack.10), calls=%async_computation.2 | async-start | bytes 4194304 | tf_op jit(solution)/shard_map/all_to_all | solution.py:57
  39.5 9.3 %all-gather.7.cloned.1.call-done = f32[16,128,128]{2,1,0:T(8,128)} async-done(((f32[4,128,128]{2,1,0:T(8,128)}), f32[16,128,128]{2,1,0:T(8,128)}) %all-gather.7.cloned.1.call-update) | async-done | bytes 1048592 | tf_op jit(solution)/shard_map/all_gather | solution.py:20
  48.8 2.0 fusion.24
  50.9 97.9 %all-to-all-done.2 = bf16[16,4,16,1024]{3,2,1,0:T(8,128)(2,1)S(1)} async-done(((bf16[16,4,16,1024]{3,2,1,0:T(8,128)(2,1)}), bf16[16,4,16,1024]{3,2,1,0:T(8,128)(2,1)S(1)}, u32[]{:S(2)}, u32[]{:S(2)}) %all-to-all-start.2) | async-done | bytes 2097184 | tf_op jit(solution)/shard_map/all_to_all | solution.py:57
  148.8 2.3 pad_maximum_fusion
  151.1 5.7 %all-to-all-start.3 = ((bf16[2,64,16,1024]{3,2,1,0:T(8,128)(2,1)}), bf16[2,64,16,1024]{3,2,1,0:T(8,128)(2,1)}, u32[]{:S(2)}, u32[]{:S(2)}) async-start(bf16[2,64,16,1024]{3,2,1,0:T(8,128)(2,1)} %pad_maximum_fusion), calls=%async_computation.3 | async-start | bytes 8388608 | tf_op jit(solution)/shard_map/all_to_all | solution.py:57
  156.9 28.5 %all-gather.5.cloned.1.call-done = f32[16,4,128,128]{3,2,1,0:T(8,128)} async-done(((f32[1,4,128,128]{3,2,1,0:T(8,128)}), f32[16,4,128,128]{3,2,1,0:T(8,128)}) %all-gather.5.cloned.1.call-update) | async-done | bytes 4194320 | tf_op jit(solution)/shard_map/all_gather | solution.py:20
  185.5 4.0 %fusion.3 = f32[512,4,128]{0,2,1:T(8,128)} fusion(f32[16,4,128,128]{3,2,1,0:T(8,128)} %all-gather.5.cloned.1.call-done, f32[1,4,128,128]{3,2,1,0:T(8,128)S(1)} %copy-done.4, f32[4,128,128]{2,1,0:T(8,128)S(1)} %copy-done.3, f32[16,128,128]{2,1,0:T(8,128)} %all-gather.7.cloned.1.call-done, f32[8,128,128]{2,1,0:T(8,128)S(1)} %all-gather, pred[]{:T(512)S(6)} %gt.66, ...), kind=kOutput, calls=%fused_computation.7 | convolution fusion | flops 70123520 | bytes 7340054 | tf_op jit(solution)/shard_map/thd,hde->the/dot_general | solution.py:99
  189.5 2.8 %multiply_reduce_fusion = (f32[512]{0:T(512)S(1)}, f32[512,4,128]{0,2,1:T(8,128)S(1)}) fusion(f32[512,4,128]{0,2,1:T(8,128)} %fusion.3, bf16[512,4,128]{0,2,1:T(8,128)(2,1)S(1)} %bitcast.78, pred[512,512]{1,0:T(8,128)(4,1)S(1)} %iota_compare_fusion, bf16[512,512]{1,0:T(8,128)(2,1)} %param.7, bf16[512,512]{1,0:T(8,128)(2,1)S(1)} %copy-done), kind=kOutput, calls=%fused_computation.14 | convolution fusion | flops 540802560 | bytes 3934208 | tf_op jit(solution)/shard_map/hts,she->the/dot_general | solution.py:84
  192.3 0.3 copy.46
  192.6 0.6 broadcast_in_dim.33
  193.2 4.8 %all-to-all-start.4 = ((f32[4,1,512]{2,1,0:T(1,128)}), f32[4,1,512]{2,1,0:T(1,128)S(1)}, u32[]{:S(2)}, u32[]{:S(2)}) async-start(f32[4,1,512]{2,1,0:T(1,128)} %broadcast_in_dim.33), calls=%async_computation.4 | async-start | bytes 16384 | tf_op jit(solution)/shard_map/all_to_all | solution.py:32
  198.6 3.3 %all-to-all-done.4 = f32[4,1,512]{2,1,0:T(1,128)S(1)} async-done(((f32[4,1,512]{2,1,0:T(1,128)}), f32[4,1,512]{2,1,0:T(1,128)S(1)}, u32[]{:S(2)}, u32[]{:S(2)}) %all-to-all-start.4) | async-done | bytes 8224 | tf_op jit(solution)/shard_map/all_to_all | solution.py:32
  201.9 1.5 broadcast_in_dim.32
  203.4 5.0 %all-to-all-start = ((bf16[4,512,512]{1,2,0:T(8,128)(2,1)}), bf16[4,512,512]{1,2,0:T(8,128)(2,1)S(1)}, u32[]{:S(2)}, u32[]{:S(2)}) async-start(bf16[4,512,512]{1,2,0:T(8,128)(2,1)} %broadcast_in_dim.32), calls=%async_computation | async-start | bytes 4194304 | tf_op jit(solution)/shard_map/all_to_all | solution.py:32
  208.5 5.0 %copy.48 = bf16[2,64,16,1024]{3,2,0,1:T(8,128)(2,1)} copy(bf16[2,64,16,1024]{3,2,1,0:T(8,128)(2,1)} %all-to-all-done.3) | data formatting | bytes 8388608 | tf_op jit(solution)/shard_map/all_to_all | solution.py:57
  213.5 12.9 %all-to-all-done = bf16[4,512,512]{1,2,0:T(8,128)(2,1)S(1)} async-done(((bf16[4,512,512]{1,2,0:T(8,128)(2,1)}), bf16[4,512,512]{1,2,0:T(8,128)(2,1)S(1)}, u32[]{:S(2)}, u32[]{:S(2)}) %all-to-all-start) | async-done | bytes 2097184 | tf_op jit(solution)/shard_map/all_to_all | solution.py:32
  226.4 5.5 %multiply_convert_fusion = bf16[512,1024]{1,0:T(8,128)(2,1)} fusion(bf16[512,2048]{0,1:T(8,128)(2,1)S(1)} %bitcast.76, bf16[2048,1024]{1,0:T(8,128)(2,1)} %bitcast.75, f32[512]{0:T(512)S(1)} %add_rsqrt_fusion), kind=kOutput, calls=%fused_computation.2 | convolution fusion | flops 2148532224 | bytes 7342080 | tf_op jit(solution)/shard_map/dot_general | solution.py:110
  (25 shorter events, 0.8 us)
Async XLA Ops:
  6.5 178.9 %copy-start = (bf16[512,512]{1,0:T(8,128)(2,1)S(1)}, bf16[512,512]{1,0:T(8,128)(2,1)}, u32[]{:S(2)}) copy-start(bf16[512,512]{1,0:T(8,128)(2,1)} %param.5) | copy-start | bytes 1572868
  6.5 5.8 %copy-start.6 = (bf16[16,1024]{1,0:T(8,128)(2,1)S(1)}, bf16[16,1024]{1,0:T(8,128)(2,1)}, u32[]{:S(2)}) copy-start(bf16[16,1024]{1,0:T(8,128)(2,1)} %param.9) | copy-start | bytes 98308
  6.5 42.2 %all-gather.7.cloned.1.call-start = ((), (), s32[]{:S(2)}) async-start(), calls=%async_computation.6 | async-start | bytes 1310720 | tf_op jit(solution)/shard_map/all_gather | solution.py:20
  7.9 16.3 %copy-start.1 = (bf16[512,512]{0,1:T(8,128)(2,1)}, bf16[512,512]{0,1:T(8,128)(2,1)S(1)}, u32[]{:S(2)}) copy-start(bf16[512,512]{0,1:T(8,128)(2,1)S(1)} %copy.52) | copy-start | bytes 1572868
  24.2 124.6 %all-to-all-start.2 = ((bf16[16,4,16,1024]{3,2,1,0:T(8,128)(2,1)}), bf16[16,4,16,1024]{3,2,1,0:T(8,128)(2,1)S(1)}, u32[]{:S(2)}, u32[]{:S(2)}) async-start(bf16[16,4,16,1024]{3,2,1,0:T(8,128)(2,1)} %stack.10), calls=%async_computation.2 | async-start | bytes 4194304 | tf_op jit(solution)/shard_map/all_to_all | solution.py:57
  39.4 146.0 %all-gather.5.cloned.1.call-start = ((), (), s32[]{:S(2)}) async-start(), calls=%async_computation.5 | async-start | bytes 4456448 | tf_op jit(solution)/shard_map/all_gather | solution.py:20
  151.1 34.3 %copy-start.3 = (f32[4,128,128]{2,1,0:T(8,128)S(1)}, f32[4,128,128]{2,1,0:T(8,128)}, u32[]{:S(2)}) copy-start(f32[4,128,128]{2,1,0:T(8,128)} %slice_add_fusion.18) | copy-start | bytes 786436
  151.1 34.3 %copy-start.4 = (f32[1,4,128,128]{3,2,1,0:T(8,128)S(1)}, f32[1,4,128,128]{3,2,1,0:T(8,128)}, u32[]{:S(2)}) copy-start(f32[1,4,128,128]{3,2,1,0:T(8,128)} %fusion.24) | copy-start | bytes 786436
  151.1 41.5 %all-to-all-start.3 = ((bf16[2,64,16,1024]{3,2,1,0:T(8,128)(2,1)}), bf16[2,64,16,1024]{3,2,1,0:T(8,128)(2,1)}, u32[]{:S(2)}, u32[]{:S(2)}) async-start(bf16[2,64,16,1024]{3,2,1,0:T(8,128)(2,1)} %pad_maximum_fusion), calls=%async_computation.3 | async-start | bytes 8388608 | tf_op jit(solution)/shard_map/all_to_all | solution.py:57
  156.9 32.6 %copy-start.2 = (bf16[512,512]{0,1:T(8,128)(2,1)S(1)}, bf16[512,512]{0,1:T(8,128)(2,1)}, u32[]{:S(2)}) copy-start(bf16[512,512]{0,1:T(8,128)(2,1)} %copy-done.1) | copy-start | bytes 1572868
  189.5 8.6 %copy-start.5 = (bf16[512,512]{1,0:T(8,128)(2,1)S(1)}, bf16[512,512]{1,0:T(8,128)(2,1)}, u32[]{:S(2)}) copy-start(bf16[512,512]{1,0:T(8,128)(2,1)} %param.8) | copy-start | bytes 1572868
  193.2 8.7 %all-to-all-start.4 = ((f32[4,1,512]{2,1,0:T(1,128)}), f32[4,1,512]{2,1,0:T(1,128)S(1)}, u32[]{:S(2)}, u32[]{:S(2)}) async-start(f32[4,1,512]{2,1,0:T(1,128)} %broadcast_in_dim.33), calls=%async_computation.4 | async-start | bytes 16384 | tf_op jit(solution)/shard_map/all_to_all | solution.py:32
  203.4 23.0 %all-to-all-start = ((bf16[4,512,512]{1,2,0:T(8,128)(2,1)}), bf16[4,512,512]{1,2,0:T(8,128)(2,1)S(1)}, u32[]{:S(2)}, u32[]{:S(2)}) async-start(bf16[4,512,512]{1,2,0:T(8,128)(2,1)} %broadcast_in_dim.32), calls=%async_computation | async-start | bytes 4194304 | tf_op jit(solution)/shard_map/all_to_all | solution.py:32
Sparse Core Ops, SparseCore 0:
  12.5 36.2 all-gather.6
  50.9 134.5 all-gather.4
